TPU v7x, 32 devices: a whole 2x2x4 slice. The times are simulated.
32 devices in a mesh: group: 4 (over y, x), dp: 8 (over z, core).
Axes of the slice: x: 2, y: 2, z: 4, core: 2. Of those that a mesh axis runs over, the one named last changes fastest.
Arguments:
- observations: bfloat16 [64, 64, 4096], P('dp', None, 'group'), may hold values from -6 to 6
- next_observations: bfloat16 [1024, 4096], P('dp', 'group'), may hold values from -6 to 6
- trunk_weights: bfloat16 [2, 4096, 4096], P(None, 'dp', 'group'), may hold values from -0.125 to 0.125
- head_weights: bfloat16 [4096, 19], P('group'), may hold values from -0.25 to 0.25
- acting_policy_logits: float32 [64, 63, 18], P('dp'), may hold values from -16 to 330, as said below
- actions: int32 [64, 63], P('dp'), may hold values from 0 to 17
- rewards: float32 [64, 63], P('dp'), may hold values from -6 to 6
- episode_finished: int32 [64, 63], P('dp'), may hold values 0 or 1
Outputs:
- trunk_grads: float32 [2, 4096, 4096], P(None, 'dp', 'group')
- head_grads: float32 [4096, 19], P(('group', 'dp'))
- actor_logits: float32 [1024, 18], P('dp')
Inputs may be any that keep to these rules, and one draw needn't show every extreme that they name: `acting_policy_logits`: Real-valued scores, one row for each step and trajectory.
All inputs are finite; a program needn't handle non-finite values. No bound on the sum of `episode_finished` on one device may be relied on, other than what follows from the above.
Results may differ from a plain program's by a relative error of at most 0.012.
Values may be sent and summed in bfloat16 or wider, within the bound.
A program may use at most 128 MiB of HBM per device.

v0:
```python
import jax
import jax.numpy as jnp
from jax import lax
from jax.sharding import PartitionSpec as P

discount_rate = 0.99
value_weight = 0.5
entropy_weight = 0.1
loss_divisor = 16.0


def contract_rows(left, right):
    return lax.dot_general(
        left, right, (((0,), (0,)), ((), ())), preferred_element_type=jnp.float32
    )


def contract_cols(left, right):
    return lax.dot_general(
        left, right, (((1,), (1,)), ((), ())), preferred_element_type=jnp.float32
    )


def silu_slope(pre_value):
    sigma = jax.nn.sigmoid(pre_value)
    return sigma * (1.0 + pre_value * (1.0 - sigma))


def importance_trace_gradients(
    learner_output, acting_policy_logits, actions, rewards, episode_finished
):
    number_of_actions = acting_policy_logits.shape[-1]
    logits = learner_output[:, :, :number_of_actions]
    values = learner_output[:, :, number_of_actions]
    log_policy = jax.nn.log_softmax(logits[:, :-1], axis=-1)
    log_behave = jax.nn.log_softmax(acting_policy_logits, axis=-1)
    chosen = (
        actions[:, :, None] == jnp.arange(number_of_actions, dtype=jnp.int32)[None, None, :]
    ).astype(jnp.float32)
    ratio = jnp.exp(jnp.sum((log_policy - log_behave) * chosen, axis=-1))
    clipped = jnp.minimum(ratio, 1.0)
    discount = discount_rate * (1.0 - episode_finished.astype(jnp.float32))
    current = values[:, :-1]
    following = values[:, 1:]
    deltas = clipped * (rewards + discount * following - current)

    def backward_step(carried, step_item):
        delta_now, factor_now = step_item
        carried = delta_now + factor_now * carried
        return (carried, carried)

    start_carry = jnp.zeros((values.shape[0],), jnp.float32)
    _, corrections = lax.scan(
        backward_step, start_carry, (deltas.T, (discount * clipped).T), reverse=True
    )
    targets = current + corrections.T
    next_targets = jnp.concatenate([targets[:, 1:], values[:, -1:]], axis=1)
    advantage = clipped * (rewards + discount * next_targets - current)
    probability = jnp.exp(log_policy)
    entropy = -jnp.sum(probability * log_policy, axis=-1)
    logit_grad = (
        -advantage[..., None] * (chosen - probability)
        + entropy_weight * probability * (log_policy + entropy[..., None])
    ) / loss_divisor
    value_grad = -value_weight * (targets - current) / loss_divisor
    step_grad = jnp.concatenate([logit_grad, value_grad[..., None]], axis=-1)
    last_row = jnp.zeros((values.shape[0], 1, number_of_actions + 1), jnp.float32)
    return jnp.concatenate([step_grad, last_row], axis=1)


def per_device(
    observations,
    next_observations,
    trunk_weights,
    head_weights,
    acting_policy_logits,
    actions,
    rewards,
    episode_finished,
):
    traj_count, step_count, feature_block = observations.shape
    learner_rows = traj_count * step_count
    number_of_actions = acting_policy_logits.shape[-1]
    layer_total = trunk_weights.shape[0]
    own_rows = observations.reshape(learner_rows, feature_block)
    gathered_weights = [
        lax.all_gather(trunk_weights[layer_index], "dp", axis=0, tiled=True)
        for layer_index in range(layer_total)
    ]
    joined = jnp.concatenate([own_rows, next_observations], axis=0)
    inputs_full = []
    products_block = []
    current = joined
    for forward_layer_index in range(layer_total):
        forward_whole = lax.all_gather(current, "group", axis=1, tiled=True)
        inputs_full.append(forward_whole)
        product = jnp.dot(
            forward_whole, gathered_weights[forward_layer_index], preferred_element_type=jnp.float32
        )
        products_block.append(product)
        current = jax.nn.silu(product).astype(jnp.bfloat16)
    partial_head = jnp.dot(current, head_weights, preferred_element_type=jnp.float32)
    totals = lax.psum(partial_head, "group")
    inputs_full, products_block, last_block, totals = (inputs_full, products_block, current, totals)
    inputs_full = [whole[:learner_rows] for whole in inputs_full]
    products_block = [block[:learner_rows] for block in products_block]
    last_block = last_block[:learner_rows]
    head_out = totals[:learner_rows]
    actor_logits = totals[learner_rows:, :number_of_actions]
    learner_output = head_out.reshape(traj_count, step_count, number_of_actions + 1)
    output_gradient = importance_trace_gradients(
        learner_output, acting_policy_logits, actions, rewards, episode_finished
    )
    output_gradient = output_gradient.reshape(learner_rows, number_of_actions + 1).astype(
        jnp.bfloat16
    )
    head_partial = contract_rows(last_block, output_gradient)
    head_grads = lax.psum_scatter(head_partial, "dp", scatter_dimension=0, tiled=True)
    input_grad = contract_cols(output_gradient, head_weights)
    grad_list = [None] * layer_total
    for layer_index in range(layer_total - 1, -1, -1):
        pre_grad = (input_grad * silu_slope(products_block[layer_index])).astype(jnp.bfloat16)
        all_inputs = lax.all_to_all(
            inputs_full[layer_index], "dp", split_axis=1, concat_axis=0, tiled=True
        )
        all_upstream = lax.all_gather(pre_grad, "dp", axis=0, tiled=True)
        grad_list[layer_index] = contract_rows(all_inputs, all_upstream)
        if layer_index > 0:
            full_grad = contract_cols(pre_grad, gathered_weights[layer_index])
            input_grad = lax.psum_scatter(full_grad, "group", scatter_dimension=1, tiled=True)
    return (jnp.stack(grad_list), head_grads, actor_logits)


def solution(mesh):
    in_specs = (
        P("dp", None, "group"),
        P("dp", "group"),
        P(None, "dp", "group"),
        P("group", None),
        P("dp", None, None),
        P("dp", None),
        P("dp", None),
        P("dp", None),
    )
    out_specs = (P(None, "dp", "group"), P(("group", "dp"), None), P("dp", None))
    return jax.shard_map(
        per_device, mesh=mesh, in_specs=in_specs, out_specs=out_specs, check_vma=False
    )
```

profile of v0, /device:TPU:0, one launch (start us, length us, event | category | flops | bytes accessed | tf_op | source)
XLA Modules:
  0.0 727.3 jit_solution(5411754395285372085)
XLA Ops:
  7.2 2.6 pad_maximum_fusion.1
  9.9 0.0 all-gather.17.cloned.1.call-start
  9.9 1.5 fusion.27
  11.5 0.0 all-gather.19.cloned.1.call-start
  11.5 0.7 all-gather.19.cloned.1.call-update
  12.3 62.2 %all-gather.9.cloned.1.call-done = bf16[640,4096]{1,0:T(8,128)(2,1)} async-done(((bf16[640,1024]{1,0:T(8,128)(2,1)}), bf16[640,4096]{1,0:T(8,128)(2,1)}) %all-gather.9.cloned.1.call-update) | async-done | bytes 5242896 | tf_op jit(solution)/shard_map/all_gather | solution.py:95
  74.5 83.7 %all-gather.17.cloned.1.call-done = bf16[1,4096,1024]{2,1,0:T(8,128)(2,1)} async-done(((bf16[1,512,1024]{2,1,0:T(8,128)(2,1)}), bf16[1,4096,1024]{2,1,0:T(8,128)(2,1)}) %all-gather.17.cloned.1.call-update) | async-done | bytes 8388624 | tf_op jit(solution)/shard_map/all_gather | solution.py:87
  158.1 10.7 %multiply_convert_fusion.1 = (bf16[640,1024]{1,0:T(8,128)(2,1)}, f32[640,1024]{1,0:T(8,128)S(1)}) fusion(bf16[640,4096]{1,0:T(8,128)(2,1)} %all-gather.9.cloned.1.call-done, bf16[1,4096,1024]{2,1,0:T(8,128)(2,1)} %all-gather.17.cloned.1.call-done), kind=kOutput, calls=%fused_computation.12 | convolution fusion | flops 5371985920 | bytes 17563648 | tf_op jit(solution)/shard_map/dot_general | solution.py:97
  168.9 0.0 reduce-scatter.3.cloned.1.call-start
  169.1 71.2 %all-gather.19.cloned.1.call-done = bf16[1,4096,1024]{2,1,0:T(8,128)(2,1)} async-done(((bf16[1,512,1024]{2,1,0:T(8,128)(2,1)}), bf16[1,4096,1024]{2,1,0:T(8,128)(2,1)}) %all-gather.19.cloned.1.call-update) | async-done | bytes 8388624 | tf_op jit(solution)/shard_map/all_gather | solution.py:87
  240.3 62.1 %all-gather.11.cloned.1.call-done = bf16[640,4096]{1,0:T(8,128)(2,1)} async-done(((bf16[640,1024]{1,0:T(8,128)(2,1)}), bf16[640,4096]{1,0:T(8,128)(2,1)}) %all-gather.11.cloned.1.call-update) | async-done | bytes 5242896 | tf_op jit(solution)/shard_map/all_gather | solution.py:95
  302.4 10.9 %multiply_convert_fusion = (bf16[640,1024]{1,0:T(8,128)(2,1)S(1)}, f32[640,1024]{1,0:T(8,128)}) fusion(bf16[640,4096]{1,0:T(8,128)(2,1)} %all-gather.11.cloned.1.call-done, bf16[1,4096,1024]{2,1,0:T(8,128)(2,1)} %all-gather.19.cloned.1.call-done), kind=kOutput, calls=%fused_computation.11 | convolution fusion | flops 5371985920 | bytes 17563648 | tf_op jit(solution)/shard_map/dot_general | solution.py:97
  313.3 1.1 copy-done.3
  314.3 0.4 fusion.28
  314.8 16.2 %psum.7 = f32[640,19]{0,1:T(8,128)S(1)} all-reduce(f32[640,19]{0,1:T(8,128)S(1)} %fusion.28), channel_id=1, replica_groups=mesh['group'=4,'dp'=8] {'group'}, use_global_device_ids=true, to_apply=%region_0.1 | all-reduce | flops 12160 | bytes 97280 | tf_op jit(solution)/shard_map/psum | solution.py:103
  331.0 0.1 reshape.32
  331.2 0.1 slice.56
  331.3 0.1 multiply_bitcast_fusion
  331.3 0.1 copy.50
  331.4 0.1 copy.49
  331.5 4.7 while.17
  336.3 0.1 copy.51
  336.4 0.1 slice.55
  336.4 0.1 fusion.25
  336.6 0.1 convert_element_type.26
  336.7 3.4 multiply_convert_fusion.3
  340.1 11.5 %fusion.2 = f32[512,4096]{1,0:T(8,128)} fusion(bf16[512,1024]{1,0:T(8,128)(2,1)} %multiply_convert_fusion.3, bf16[1,4096,1024]{2,1,0:T(8,128)(2,1)} %all-gather.19.cloned.1.call-done), kind=kOutput, calls=%fused_computation.3 | convolution fusion | flops 4294967296 | bytes 17825792 | tf_op jit(solution)/shard_map/dot_general | solution.py:19
  351.7 0.5 all-gather.15.cloned.1.call-update
  352.3 4.7 slice.62
  357.0 6.6 copy.47
  363.6 4.6 all-to-all-start
  368.2 0.2 all-gather.13.cloned.1.call-start
  368.4 69.6 %reduce-scatter.3.cloned.1.call-done = f32[512,1024]{1,0:T(8,128)} async-done(((f32[512,4096]{1,0:T(8,128)}), f32[512,1024]{1,0:T(8,128)}) %reduce-scatter.3.cloned.1.call-update) | async-done | bytes 2097168 | tf_op jit(solution)/shard_map/reduce_scatter | solution.py:130
  438.0 3.3 multiply_convert_fusion.2
  441.3 2.2 slice-done
  443.5 2.4 copy.55
  445.9 50.0 %all-to-all-done = bf16[512,8,512]{0,2,1:T(8,128)(2,1)} async-done(((bf16[512,8,512]{0,2,1:T(8,128)(2,1)}), bf16[512,8,512]{0,2,1:T(8,128)(2,1)}, u32[]{:S(2)}, u32[]{:S(2)}) %all-to-all-start) | async-done | bytes 4194336 | tf_op jit(solution)/shard_map/all_to_all | solution.py:123
  495.9 4.6 all-to-all-start.1
  500.5 0.0 reduce-scatter.5.cloned.1.call-start
  500.5 6.6 copy.48
  507.2 0.6 slice.70
  507.8 0.9 fusion.8
  508.7 146.3 %all-to-all-done.1 = bf16[512,8,512]{2,0,1:T(8,128)(2,1)} async-done(((bf16[512,8,512]{2,0,1:T(8,128)(2,1)}), bf16[512,8,512]{2,0,1:T(8,128)(2,1)}, u32[]{:S(2)}, u32[]{:S(2)}) %all-to-all-start.1) | async-done | bytes 4194336 | tf_op jit(solution)/shard_map/all_to_all | solution.py:123
  655.0 8.3 %convolution_bitcast_fusion = f32[1,512,1024]{2,1,0:T(8,128)S(1)} fusion(bf16[4096,512]{1,0:T(8,128)(2,1)} %bitcast.13, bf16[4096,1024]{1,0:T(8,128)(2,1)} %all-gather.15.cloned.1.call-done), kind=kOutput, calls=%fused_computation.15 | convolution fusion | flops 4294967296 | bytes 14680064 | tf_op jit(solution)/shard_map/dot_general | solution.py:13
  663.3 26.0 %all-gather.13.cloned.1.call-done = bf16[4096,1024]{1,0:T(8,128)(2,1)} async-done(((bf16[512,1024]{1,0:T(8,128)(2,1)}), bf16[4096,1024]{1,0:T(8,128)(2,1)}) %all-gather.13.cloned.1.call-update) | async-done | bytes 8388624 | tf_op jit(solution)/shard_map/all_gather | solution.py:126
  689.3 8.2 %convolution_bitcast_fusion.1 = f32[1,512,1024]{2,1,0:T(8,128)S(1)} fusion(bf16[4096,512]{1,0:T(8,128)(2,1)} %bitcast.68, bf16[4096,1024]{1,0:T(8,128)(2,1)} %all-gather.13.cloned.1.call-done), kind=kOutput, calls=%fused_computation.16 | convolution fusion | flops 4294967296 | bytes 14680064 | tf_op jit(solution)/shard_map/dot_general | solution.py:13
  697.5 2.5 pad_maximum_fusion
  700.0 20.5 %reduce-scatter.5.cloned.1.call-done = f32[128,19]{0,1:T(8,128)} async-done(((f32[1024,19]{0,1:T(8,128)}), f32[128,19]{0,1:T(8,128)}) %reduce-scatter.5.cloned.1.call-update) | async-done | bytes 9744 | tf_op jit(solution)/shard_map/reduce_scatter | solution.py:118
  (169 shorter events, 4.2 us)
Async XLA Ops:
  7.2 307.2 %copy-start = (bf16[1024,19]{0,1:T(8,128)(2,1)S(1)}, bf16[1024,19]{0,1:T(8,128)(2,1)}, u32[]{:S(2)}) copy-start(bf16[1024,19]{0,1:T(8,128)(2,1)} %param.14) | copy-start | bytes 116740
  7.2 2.7 copy-start.2
  7.2 67.3 %all-gather.9.cloned.1.call-start = ((), (), s32[]{:S(2)}) async-start(), calls=%async_computation.4 | async-start | bytes 6553600 | tf_op jit(solution)/shard_map/all_gather | solution.py:95
  9.9 148.3 %all-gather.17.cloned.1.call-start = ((), (), s32[]{:S(2)}) async-start(), calls=%async_computation.10 | async-start | bytes 9437184 | tf_op jit(solution)/shard_map/all_gather | solution.py:87
  11.5 228.8 %all-gather.19.cloned.1.call-start = ((), (), s32[]{:S(2)}) async-start(), calls=%async_computation.11 | async-start | bytes 9437184 | tf_op jit(solution)/shard_map/all_gather | solution.py:87
  12.2 156.8 %copy-start.5 = (f32[8,63,18]{1,0,2:T(8,128)S(1)}, f32[8,63,18]{1,0,2:T(8,128)}, u32[]{:S(2)}) copy-start(f32[8,63,18]{1,0,2:T(8,128)} %param.15) | copy-start | bytes 108868
  12.2 290.2 %all-gather.11.cloned.1.call-start = ((), (), s32[]{:S(2)}) async-start(), calls=%async_computation.5 | async-start | bytes 6553600 | tf_op jit(solution)/shard_map/all_gather | solution.py:95
  168.9 269.1 %reduce-scatter.3.cloned.1.call-start = ((), (), s32[]{:S(2)}) async-start(), calls=%async_computation.6 | async-start | bytes 10485760 | tf_op jit(solution)/shard_map/reduce_scatter | solution.py:130
  169.0 162.1 %copy-start.8 = (s32[8,63]{1,0:T(8,128)S(1)}, s32[8,63]{1,0:T(8,128)}, u32[]{:S(2)}) copy-start(s32[8,63]{1,0:T(8,128)} %param.16) | copy-start | bytes 6052
  169.0 162.2 %copy-start.6 = (s32[8,63]{1,0:T(8,128)S(1)}, s32[8,63]{1,0:T(8,128)}, u32[]{:S(2)}) copy-start(s32[8,63]{1,0:T(8,128)} %param.18) | copy-start | bytes 6052
  169.0 162.2 %copy-start.7 = (f32[8,63]{1,0:T(8,128)S(1)}, f32[8,63]{1,0:T(8,128)}, u32[]{:S(2)}) copy-start(f32[8,63]{1,0:T(8,128)} %param.17) | copy-start | bytes 6052
  313.3 1.1 copy-start.3
  351.7 303.3 %all-gather.15.cloned.1.call-start = ((), (), s32[]{:S(2)}) async-start(), calls=%async_computation.8 | async-start | bytes 9437184 | tf_op jit(solution)/shard_map/all_gather | solution.py:126
  363.6 132.3 %all-to-all-start = ((bf16[512,8,512]{0,2,1:T(8,128)(2,1)}), bf16[512,8,512]{0,2,1:T(8,128)(2,1)}, u32[]{:S(2)}, u32[]{:S(2)}) async-start(bf16[512,8,512]{0,2,1:T(8,128)(2,1)} %bitcast.65), calls=%async_computation | async-start | bytes 8388608 | tf_op jit(solution)/shard_map/all_to_all | solution.py:123
  368.2 321.1 %all-gather.13.cloned.1.call-start = ((), (), s32[]{:S(2)}) async-start(), calls=%async_computation.7 | async-start | bytes 9437184 | tf_op jit(solution)/shard_map/all_gather | solution.py:126
  441.3 2.2 slice-start
  495.9 159.1 %all-to-all-start.1 = ((bf16[512,8,512]{2,0,1:T(8,128)(2,1)}), bf16[512,8,512]{2,0,1:T(8,128)(2,1)}, u32[]{:S(2)}, u32[]{:S(2)}) async-start(bf16[512,8,512]{2,0,1:T(8,128)(2,1)} %bitcast.66), calls=%async_computation.2 | async-start | bytes 8388608 | tf_op jit(solution)/shard_map/all_to_all | solution.py:123
  500.5 220.0 %reduce-scatter.5.cloned.1.call-start = ((), (), s32[]{:S(2)}) async-start(), calls=%async_computation.9 | async-start | bytes 110592 | tf_op jit(solution)/shard_map/reduce_scatter | solution.py:118
  500.5 7.3 copy-start.4
  689.3 31.2 %copy-start.1 = (bf16[1024,19]{0,1:T(8,128)(2,1)S(1)}, bf16[1024,19]{0,1:T(8,128)(2,1)}, u32[]{:S(2)}) copy-start(bf16[1024,19]{0,1:T(8,128)(2,1)} %param.14) | copy-start | bytes 116740
Sparse Core Ops, SparseCore 0:
  10.4 64.0 all-gather.8
  76.1 82.0 all-gather.16
  159.7 80.5 all-gather.18
  242.6 59.7 all-gather.10
  351.8 86.1 reduce-scatter.2
  439.4 153.6 all-gather.14
  594.7 94.5 all-gather.12
  692.1 28.3 reduce-scatter.4
where the time goes:
time: 728 us; the launch traced here: 727 us
  waiting for transfers between devices  593 us (81%)
  matrix products  54.4 us (7%)
  local copies, waits for them, and re-layouts  28.9 us (4%)
  blocking collectives  16.2 us (2%)
  between operations  14.3 us (2%)
  other arithmetic  9.97 us (1%)
  starting transfers between devices  9.68 us (1%)
    all_to_all x2, waiting for transfers between devices, per_device(): lax.all_to_all(inputs_full[layer_index], 'dp', split_axis=1, concat_axis=...  196 us
    all_gather x2, waiting for transfers between devices, per_device(): lax.all_gather(trunk_weights[layer_index], 'dp', axis=0, tiled=True)  155 us
    all_gather x2, waiting for transfers between devices, per_device(): forward_whole = lax.all_gather(current, 'group', axis=1, tiled=True)  124 us
    reduce_scatter x1, waiting for transfers between devices, per_device(): lax.psum_scatter(full_grad, 'group', scatter_dimension=1, tiled=True)  69.6 us
    all_gather x2, waiting for transfers between devices, per_device(): all_upstream = lax.all_gather(pre_grad, 'dp', axis=0, tiled=True)  26 us
    dot_general x2, matrix products, per_device(): jnp.dot(forward_whole, gathered_weights[forward_layer_index], preferred_e...  21.6 us
    reduce_scatter x1, waiting for transfers between devices, per_device(): lax.psum_scatter(head_partial, 'dp', scatter_dimension=0, tiled=True)  20.5 us
    dot_general x3, matrix products, contract_rows(): lax.dot_general(left, right, (((0,), (0,)), ((), ())), preferred_element_...  17.4 us
  transfers between devices with their start and end apart: 10, of which 9 were waited for; matrix products, arithmetic and copies ran while one was open for 8% of the time, Pallas kernels for 0%

commit v1 on v0

--- a/solution.py
+++ b/solution.py
@@ -120,9 +120,10 @@
     grad_list = [None] * layer_total
     for layer_index in range(layer_total - 1, -1, -1):
         pre_grad = (input_grad * silu_slope(products_block[layer_index])).astype(jnp.bfloat16)
-        all_inputs = lax.all_to_all(
-            inputs_full[layer_index], "dp", split_axis=1, concat_axis=0, tiled=True
-        )
+        own = inputs_full[layer_index]
+        parts = jnp.split(own, lax.axis_size("dp"), axis=1)
+        received = lax.all_to_all(jnp.stack(parts), "dp", 0, 0)
+        all_inputs = jnp.concatenate(received, axis=0)
         all_upstream = lax.all_gather(pre_grad, "dp", axis=0, tiled=True)
         grad_list[layer_index] = contract_rows(all_inputs, all_upstream)
         if layer_index > 0:

time: 728 us -> 793 us (1.089)
  waiting for transfers between devices: 593 us -> 650 us
    all_to_all x2, waiting for transfers between devices: 196 us -> 282 us  [per_device(): received = lax.all_to_all(jnp.stack(parts), 'dp', 0, 0)]
    unnamed x20 -> x34, local copies, waits for them, and re-layouts: 1.31 us -> 27.7 us
    all_gather x2, waiting for transfers between devices: 26 us -> 0.02 us  [per_device(): all_upstream = lax.all_gather(pre_grad, 'dp', axis=0, tiled=True)]
    slice x4 -> x0, local copies, waits for them, and re-layouts: 13.5 us -> none  [per_device(): inputs_full = [whole[:learner_rows] for whole in inputs_full]]
    reduce_scatter x1, waiting for transfers between devices: 20.5 us -> 7.62 us  [per_device(): lax.psum_scatter(head_partial, 'dp', scatter_dimension=0, tiled=True)]
    reduce_scatter x1, waiting for transfers between devices: 69.6 us -> 80 us  [per_device(): lax.psum_scatter(full_grad, 'group', scatter_dimension=1, tiled=True)]
    all_to_all x2 -> x0, local copies, waits for them, and re-layouts: 9.06 us -> none  [per_device(): lax.all_to_all(inputs_full[layer_index], 'dp', split_axis=1, concat_axis=...]
  transfers between devices with their start and end apart: 10 -> 10, of which waited for: 9 -> 8; matrix products, arithmetic and copies ran while one was open for 8% -> 8% of each run, Pallas kernels for 0% -> 0%
where the time goes in v1:
time: 793 us; the launch traced here: 792 us
  waiting for transfers between devices  650 us (82%)
  matrix products  54.4 us (7%)
  local copies, waits for them, and re-layouts  36.5 us (5%)
  blocking collectives  16.2 us (2%)
  between operations  14.3 us (2%)
  other arithmetic  9.99 us (1%)
  starting transfers between devices  9.61 us (1%)
    all_to_all x2, waiting for transfers between devices, per_device(): received = lax.all_to_all(jnp.stack(parts), 'dp', 0, 0)  282 us
    all_gather x2, waiting for transfers between devices, per_device(): lax.all_gather(trunk_weights[layer_index], 'dp', axis=0, tiled=True)  155 us
    all_gather x2, waiting for transfers between devices, per_device(): forward_whole = lax.all_gather(current, 'group', axis=1, tiled=True)  124 us
    reduce_scatter x1, waiting for transfers between devices, per_device(): lax.psum_scatter(full_grad, 'group', scatter_dimension=1, tiled=True)  80 us
    unnamed x34, local copies, waits for them, and re-layouts  27.7 us
    dot_general x2, matrix products, per_device(): jnp.dot(forward_whole, gathered_weights[forward_layer_index], preferred_e...  21.6 us
    dot_general x3, matrix products, contract_rows(): lax.dot_general(left, right, (((0,), (0,)), ((), ())), preferred_element_...  17.4 us
    psum x1, blocking collectives, per_device(): totals = lax.psum(partial_head, 'group')  16.2 us
  transfers between devices with their start and end apart: 10, of which 8 were waited for; matrix products, arithmetic and copies ran while one was open for 8% of the time, Pallas kernels for 0%

profile of v1, /device:TPU:0, one launch (start us, length us, event | category | flops | bytes accessed | tf_op | source)
XLA Modules:
  0.0 792.2 jit_solution(13268909748593313328)
XLA Ops:
  7.2 2.6 pad_maximum_fusion.1
  9.9 1.5 fusion.43
  11.5 0.7 all-gather.19.cloned.1.call-update
  12.3 62.2 %all-gather.9.cloned.1.call-done = bf16[640,4096]{1,0:T(8,128)(2,1)} async-done(((bf16[640,1024]{1,0:T(8,128)(2,1)}), bf16[640,4096]{1,0:T(8,128)(2,1)}) %all-gather.9.cloned.1.call-update) | async-done | bytes 5242896 | tf_op jit(solution)/shard_map/all_gather | solution.py:95
  74.5 83.7 %all-gather.17.cloned.1.call-done = bf16[1,4096,1024]{2,1,0:T(8,128)(2,1)} async-done(((bf16[1,512,1024]{2,1,0:T(8,128)(2,1)}), bf16[1,4096,1024]{2,1,0:T(8,128)(2,1)}) %all-gather.17.cloned.1.call-update) | async-done | bytes 8388624 | tf_op jit(solution)/shard_map/all_gather | solution.py:87
  158.1 10.7 %multiply_convert_fusion.1 = (bf16[640,1024]{1,0:T(8,128)(2,1)}, f32[640,1024]{1,0:T(8,128)S(1)}) fusion(bf16[640,4096]{1,0:T(8,128)(2,1)} %all-gather.9.cloned.1.call-done, bf16[1,4096,1024]{2,1,0:T(8,128)(2,1)} %all-gather.17.cloned.1.call-done), kind=kOutput, calls=%fused_computation.11 | convolution fusion | flops 5371985920 | bytes 17563648 | tf_op jit(solution)/shard_map/dot_general | solution.py:97
  169.1 71.2 %all-gather.19.cloned.1.call-done = bf16[1,4096,1024]{2,1,0:T(8,128)(2,1)} async-done(((bf16[1,512,1024]{2,1,0:T(8,128)(2,1)}), bf16[1,4096,1024]{2,1,0:T(8,128)(2,1)}) %all-gather.19.cloned.1.call-update) | async-done | bytes 8388624 | tf_op jit(solution)/shard_map/all_gather | solution.py:87
  240.3 62.1 %all-gather.11.cloned.1.call-done = bf16[640,4096]{1,0:T(8,128)(2,1)} async-done(((bf16[640,1024]{1,0:T(8,128)(2,1)}), bf16[640,4096]{1,0:T(8,128)(2,1)}) %all-gather.11.cloned.1.call-update) | async-done | bytes 5242896 | tf_op jit(solution)/shard_map/all_gather | solution.py:95
  302.4 10.9 %multiply_convert_fusion = (bf16[640,1024]{1,0:T(8,128)(2,1)S(1)}, f32[640,1024]{1,0:T(8,128)}) fusion(bf16[640,4096]{1,0:T(8,128)(2,1)} %all-gather.11.cloned.1.call-done, bf16[1,4096,1024]{2,1,0:T(8,128)(2,1)} %all-gather.19.cloned.1.call-done), kind=kOutput, calls=%fused_computation.10 | convolution fusion | flops 5371985920 | bytes 17563648 | tf_op jit(solution)/shard_map/dot_general | solution.py:97
  313.3 1.1 copy-done.3
  314.3 0.4 fusion.44
  314.8 16.2 %psum.7 = f32[640,19]{0,1:T(8,128)S(1)} all-reduce(f32[640,19]{0,1:T(8,128)S(1)} %fusion.44), channel_id=1, replica_groups=mesh['group'=4,'dp'=8] {'group'}, use_global_device_ids=true, to_apply=%region_0.1 | all-reduce | flops 12160 | bytes 97280 | tf_op jit(solution)/shard_map/psum | solution.py:103
  330.9 0.1 reshape.33
  331.3 0.1 copy.18
  331.4 0.1 copy.19
  331.5 4.7 while.17
  336.6 0.1 convert_element_type.26
  336.7 3.4 multiply_convert_fusion.3
  340.1 11.5 %fusion.2 = f32[512,4096]{1,0:T(8,128)} fusion(bf16[512,1024]{1,0:T(8,128)(2,1)} %multiply_convert_fusion.3, bf16[1,4096,1024]{2,1,0:T(8,128)(2,1)} %all-gather.19.cloned.1.call-done), kind=kOutput, calls=%fused_computation.3 | convolution fusion | flops 4294967296 | bytes 17825792 | tf_op jit(solution)/shard_map/dot_general | solution.py:19
  351.7 0.5 all-gather.15.cloned.1.call-update
  352.3 1.9 fusion.17
  354.1 1.9 fusion.16
  356.0 1.9 fusion.15
  357.9 80.0 %reduce-scatter.3.cloned.1.call-done = f32[512,1024]{1,0:T(8,128)} async-done(((f32[512,4096]{1,0:T(8,128)}), f32[512,1024]{1,0:T(8,128)}) %reduce-scatter.3.cloned.1.call-update) | async-done | bytes 2097168 | tf_op jit(solution)/shard_map/reduce_scatter | solution.py:131
  437.9 3.4 multiply_convert_fusion.2
  441.3 1.9 fusion.14
  443.1 1.9 fusion.13
  445.0 1.9 fusion.12
  446.9 1.9 fusion.11
  448.9 1.9 fusion.10
  450.8 4.7 all-to-all-start.1
  455.5 1.9 fusion.25
  457.4 1.9 fusion.24
  459.3 1.9 fusion.23
  461.2 1.9 fusion.22
  463.1 1.9 fusion.21
  465.0 1.9 fusion.20
  466.9 1.9 fusion.19
  468.7 1.9 fusion.18
  470.6 138.9 %all-to-all-done.1 = bf16[8,512,512]{2,1,0:T(8,128)(2,1)} async-done(((bf16[8,512,512]{2,1,0:T(8,128)(2,1)}), bf16[8,512,512]{2,1,0:T(8,128)(2,1)}, u32[]{:S(2)}, u32[]{:S(2)}) %all-to-all-start.1) | async-done | bytes 4194336 | tf_op jit(solution)/shard_map/all_to_all | solution.py:125
  609.5 4.5 all-to-all-start
  614.1 0.6 slice.78
  614.7 0.9 fusion.8
  615.6 8.3 %convolution_bitcast_fusion = f32[1,512,1024]{2,1,0:T(8,128)S(1)} fusion(bf16[4096,512]{1,0:T(8,128)(2,1)} %bitcast.26, bf16[4096,1024]{1,0:T(8,128)(2,1)} %all-gather.15.cloned.1.call-done), kind=kOutput, calls=%fused_computation.14 | convolution fusion | flops 4294967296 | bytes 14680064 | tf_op jit(solution)/shard_map/dot_general | solution.py:13
  623.9 143.1 %all-to-all-done = bf16[8,512,512]{2,1,0:T(8,128)(2,1)} async-done(((bf16[8,512,512]{2,1,0:T(8,128)(2,1)}), bf16[8,512,512]{2,1,0:T(8,128)(2,1)}, u32[]{:S(2)}, u32[]{:S(2)}) %all-to-all-start) | async-done | bytes 4194336 | tf_op jit(solution)/shard_map/all_to_all | solution.py:125
  767.0 8.2 %convolution_bitcast_fusion.1 = f32[1,512,1024]{2,1,0:T(8,128)S(1)} fusion(bf16[4096,512]{1,0:T(8,128)(2,1)} %bitcast.9, bf16[4096,1024]{1,0:T(8,128)(2,1)} %all-gather.13.cloned.1.call-done), kind=kOutput, calls=%fused_computation.15 | convolution fusion | flops 4294967296 | bytes 14680064 | tf_op jit(solution)/shard_map/dot_general | solution.py:13
  775.3 2.5 pad_maximum_fusion
  777.7 7.6 reduce-scatter.5.cloned.1.call-done
  (179 shorter events, 4.8 us)
Async XLA Ops:
  7.2 307.1 %copy-start = (bf16[1024,19]{0,1:T(8,128)(2,1)S(1)}, bf16[1024,19]{0,1:T(8,128)(2,1)}, u32[]{:S(2)}) copy-start(bf16[1024,19]{0,1:T(8,128)(2,1)} %param.14) | copy-start | bytes 116740
  7.2 2.7 copy-start.2
  7.2 67.3 %all-gather.9.cloned.1.call-start = ((), (), s32[]{:S(2)}) async-start(), calls=%async_computation.4 | async-start | bytes 6553600 | tf_op jit(solution)/shard_map/all_gather | solution.py:95
  9.9 148.3 %all-gather.17.cloned.1.call-start = ((), (), s32[]{:S(2)}) async-start(), calls=%async_computation.10 | async-start | bytes 9437184 | tf_op jit(solution)/shard_map/all_gather | solution.py:87
  11.5 228.8 %all-gather.19.cloned.1.call-start = ((), (), s32[]{:S(2)}) async-start(), calls=%async_computation.11 | async-start | bytes 9437184 | tf_op jit(solution)/shard_map/all_gather | solution.py:87
  12.2 156.8 %copy-start.5 = (f32[8,63,18]{1,0,2:T(8,128)S(1)}, f32[8,63,18]{1,0,2:T(8,128)}, u32[]{:S(2)}) copy-start(f32[8,63,18]{1,0,2:T(8,128)} %param.15) | copy-start | bytes 108868
  12.2 290.2 %all-gather.11.cloned.1.call-start = ((), (), s32[]{:S(2)}) async-start(), calls=%async_computation.5 | async-start | bytes 6553600 | tf_op jit(solution)/shard_map/all_gather | solution.py:95
  168.9 269.0 %reduce-scatter.3.cloned.1.call-start = ((), (), s32[]{:S(2)}) async-start(), calls=%async_computation.6 | async-start | bytes 10485760 | tf_op jit(solution)/shard_map/reduce_scatter | solution.py:131
  169.0 162.2 %copy-start.8 = (s32[8,63]{1,0:T(8,128)S(1)}, s32[8,63]{1,0:T(8,128)}, u32[]{:S(2)}) copy-start(s32[8,63]{1,0:T(8,128)} %param.16) | copy-start | bytes 6052
  169.0 162.2 %copy-start.6 = (s32[8,63]{1,0:T(8,128)S(1)}, s32[8,63]{1,0:T(8,128)}, u32[]{:S(2)}) copy-start(s32[8,63]{1,0:T(8,128)} %param.18) | copy-start | bytes 6052
  169.0 162.2 %copy-start.7 = (f32[8,63]{1,0:T(8,128)S(1)}, f32[8,63]{1,0:T(8,128)}, u32[]{:S(2)}) copy-start(f32[8,63]{1,0:T(8,128)} %param.17) | copy-start | bytes 6052
  313.3 1.1 copy-start.3
  351.6 264.0 %all-gather.15.cloned.1.call-start = ((), (), s32[]{:S(2)}) async-start(), calls=%async_computation.8 | async-start | bytes 9437184 | tf_op jit(solution)/shard_map/all_gather | solution.py:127
  352.2 414.8 %all-gather.13.cloned.1.call-start = ((), (), s32[]{:S(2)}) async-start(), calls=%async_computation.7 | async-start | bytes 9437184 | tf_op jit(solution)/shard_map/all_gather | solution.py:127
  450.8 158.7 %all-to-all-start.1 = ((bf16[8,512,512]{2,1,0:T(8,128)(2,1)}), bf16[8,512,512]{2,1,0:T(8,128)(2,1)}, u32[]{:S(2)}, u32[]{:S(2)}) async-start(bf16[8,512,512]{2,1,0:T(8,128)(2,1)} %fusion.10), calls=%async_computation.2 | async-start | bytes 8388608 | tf_op jit(solution)/shard_map/all_to_all | solution.py:125
  470.6 144.1 %copy-start.4 = (bf16[640,1024]{1,0:T(8,128)(2,1)S(1)}, bf16[640,1024]{1,0:T(8,128)(2,1)}, u32[]{:S(2)}) copy-start(bf16[640,1024]{1,0:T(8,128)(2,1)} %copy-done.3) | copy-start | bytes 3932164
  609.5 157.5 %all-to-all-start = ((bf16[8,512,512]{2,1,0:T(8,128)(2,1)}), bf16[8,512,512]{2,1,0:T(8,128)(2,1)}, u32[]{:S(2)}, u32[]{:S(2)}) async-start(bf16[8,512,512]{2,1,0:T(8,128)(2,1)} %fusion.18), calls=%async_computation | async-start | bytes 8388608 | tf_op jit(solution)/shard_map/all_to_all | solution.py:125
  614.0 171.3 %reduce-scatter.5.cloned.1.call-start = ((), (), s32[]{:S(2)}) async-start(), calls=%async_computation.9 | async-start | bytes 110592 | tf_op jit(solution)/shard_map/reduce_scatter | solution.py:118
  767.0 18.3 %copy-start.1 = (bf16[1024,19]{0,1:T(8,128)(2,1)S(1)}, bf16[1024,19]{0,1:T(8,128)(2,1)}, u32[]{:S(2)}) copy-start(bf16[1024,19]{0,1:T(8,128)(2,1)} %param.14) | copy-start | bytes 116740
Sparse Core Ops, SparseCore 0:
  10.4 64.0 all-gather.8
  76.1 82.0 all-gather.16
  159.7 80.5 all-gather.18
  242.6 59.7 all-gather.10
  351.8 86.0 reduce-scatter.2
  439.3 157.2 all-gather.14
  598.2 155.3 all-gather.12
  756.4 28.8 reduce-scatter.4
